TPU v7x, 512 devices: a 4x2x32 block of a 4x8x32 slice. The times are simulated.
512 devices in a mesh: member: 2 (over y), lon: 128 (over z, x), lat: 2 (over core).
Axes of the slice: x: 4, y: 2, z: 32, core: 2. Of those that a mesh axis runs over, the one named last changes fastest.
The devices are a block of a 4x8x32 slice.
Arguments:
- state_tokens: bfloat16 [8, 24, 1536, 768], P('member', 'lat', 'lon'), parts along dimension 0, may hold values from -32 to 32
- land_mask: int32 [24, 1536], P('lat', 'lon'), may hold values 0 or 1
- pad_mask: int32 [24], replicated, may hold values from 0 to 1, as said below
- land_embed: float32 [2, 768], replicated, may hold values from -3 to 3
- w_qkv: bfloat16 [768, 1152], replicated, may hold values from -0.21875 to 0.21875
- w_proj: bfloat16 [384, 768], replicated, may hold values from -0.3125 to 0.3125
- proj_bias: float32 [768], replicated, may hold values from -4 to 4
- norm_gain: float32 [768], replicated, may hold values from 0.5 to 1.5
- norm_shift: float32 [768], replicated, may hold values from -1.5 to 1.5
- bias_table: bfloat16 [4, 2, 12, 3312], P('lat'), may hold values from -3.5 to 320
- index_table: int32 [144, 144], replicated, may hold values from 0 to 3311
Outputs:
- result: bfloat16 [8, 24, 1536, 768], P('member', 'lat', 'lon'), parts along dimension 0
There are 2 independent parts, one for each index of `member`. A program takes and returns all parts, laid end to end along the dimension named above; an argument that names none is the same for every part. Nothing has to cross between parts.
Inputs may be any that keep to these rules, and one draw needn't show every extreme that they name: pad_mask is 1 on every row except at most the first 2 and the last 2 of the 24 rows, which are 0 where padded; one of the two ends has exactly 2 padding rows.
All inputs are finite; a program needn't handle non-finite values. No bound on the sum of `land_mask` on one device may be relied on, other than what follows from the above.
Results may differ from a plain program's by a relative error of at most 0.0085.
Values may be sent and summed in bfloat16 or wider, within the bound.
A program may use at most 64 MiB of HBM per device.

v0:
```python
import jax
import jax.numpy as jnp
from jax import lax
from jax.sharding import PartitionSpec as P

HEADS = 12
HEAD_DIM = 32
WIN_Z = 2
WIN_LAT = 6
WIN_LON = 12
WIN_TOK = 144


norm_epsilon = 1e-05


def from_behind(shard, axis, by):
    size = lax.axis_size(axis)
    return lax.ppermute(shard, axis, [(i, (i + by) % size) for i in range(size)])


def region_of(position, length, window):
    half_window = window // 2
    return jnp.where(
        position < length - window, 0, jnp.where(position < length - half_window, 1, 2)
    ).astype(jnp.int32)


def window_rules(levels, lat_start, lat_rows, lat_total, pad_mask):
    tokens = jnp.arange(WIN_TOK, dtype=jnp.int32)
    level_offset = tokens // (WIN_LAT * WIN_LON)
    row_offset = tokens // WIN_LON % WIN_LAT
    level_index = (
        jnp.arange(levels // WIN_Z, dtype=jnp.int32)[:, None] * WIN_Z + level_offset[None, :]
    )
    row_index = (
        lat_start
        + jnp.arange(lat_rows // WIN_LAT, dtype=jnp.int32)[:, None] * WIN_LAT
        + row_offset[None, :]
    )
    region = (
        region_of(level_index, levels, WIN_Z)[:, None, :] * 3
        + region_of(row_index, lat_total, WIN_LAT)[None, :, :]
    )
    source_row = (row_index + WIN_LAT // 2) % lat_total
    lookup = (
        source_row[:, :, None] == jnp.arange(lat_total, dtype=jnp.int32)[None, None, :]
    ).astype(jnp.int32)
    usable = jnp.sum(lookup * pad_mask[None, None, :], axis=-1) == 1
    return (region[:, :, :, None] == region[:, :, None, :]) & usable[None, :, None, :]


def earth_bias(bias_table, index_table):
    lat_windows, z_windows, heads, positions = bias_table.shape
    table_rows = bias_table.reshape(lat_windows * z_windows * heads, positions).T
    picked = jnp.take(table_rows, index_table.reshape(-1), axis=0)
    picked = picked.reshape(WIN_TOK, WIN_TOK, lat_windows, z_windows, heads).astype(jnp.float32)
    return jnp.transpose(picked, (3, 2, 4, 0, 1))


def to_windows(layout):
    levels, lat_rows, lon_columns, channels = layout.shape
    shaped = layout.reshape(
        levels // WIN_Z,
        WIN_Z,
        lat_rows // WIN_LAT,
        WIN_LAT,
        lon_columns // WIN_LON,
        WIN_LON,
        channels,
    )
    shaped = shaped.transpose(0, 2, 4, 1, 3, 5, 6)
    return shaped.reshape(
        levels // WIN_Z, lat_rows // WIN_LAT, lon_columns // WIN_LON, WIN_TOK, channels
    )


def from_windows(window_tiles):
    z_windows, lat_windows, lon_windows, tokens, channels = window_tiles.shape
    shaped = window_tiles.reshape(
        z_windows, lat_windows, lon_windows, WIN_Z, WIN_LAT, WIN_LON, channels
    )
    shaped = shaped.transpose(0, 3, 1, 4, 2, 5, 6)
    return shaped.reshape(z_windows * WIN_Z, lat_windows * WIN_LAT, lon_windows * WIN_LON, channels)


def attend(windows, bias_full, allowed):
    pieces = windows.reshape(windows.shape[:-1] + (3, HEADS, HEAD_DIM))
    queries = pieces[..., 0, :, :]
    key_rows = pieces[..., 1, :, :]
    value_rows = pieces[..., 2, :, :]
    scores = jnp.einsum(
        "abcthd,abcuhd->abchtu", queries, key_rows, preferred_element_type=jnp.float32
    )
    scores = scores / jnp.sqrt(jnp.float32(HEAD_DIM)) + bias_full[:, :, None]
    scores = jnp.where(allowed[:, :, None, None], scores, -jnp.inf)
    largest = jnp.max(scores, axis=-1, keepdims=True)
    powers = jnp.exp(scores - largest)
    weights = (powers / jnp.sum(powers, axis=-1, keepdims=True)).astype(jnp.bfloat16)
    attended = jnp.einsum(
        "abchtu,abcuhd->abcthd", weights, value_rows, preferred_element_type=jnp.float32
    ).astype(jnp.bfloat16)
    return attended.reshape(attended.shape[:4] + (HEADS * HEAD_DIM,))


def finish(attended, w_proj, proj_bias, norm_gain, norm_shift):
    projected = jnp.dot(attended, w_proj, preferred_element_type=jnp.float32) + proj_bias
    average = jnp.mean(projected, axis=-1, keepdims=True)
    centered = projected - average
    spread = jnp.mean(centered * centered, axis=-1, keepdims=True)
    return centered * lax.rsqrt(spread + norm_epsilon) * norm_gain + norm_shift


def on_device(
    state_tokens,
    land_mask,
    pad_mask,
    land_embed,
    w_qkv,
    w_proj,
    proj_bias,
    norm_gain,
    norm_shift,
    bias_table,
    index_table,
):
    levels, lat_rows, lon_columns, features = state_tokens.shape
    lat_total = lat_rows * lax.axis_size("lat")
    lat_start = lax.axis_index("lat") * lat_rows
    level_half = WIN_Z // 2
    lat_half = WIN_LAT // 2
    lon_half = WIN_LON // 2
    embedded = jnp.where(land_mask[:, :, None] == 1, land_embed[1], land_embed[0])
    hidden = (state_tokens.astype(jnp.float32) + embedded[None]).astype(jnp.bfloat16)
    own_rows = jnp.dot(hidden, w_qkv, preferred_element_type=jnp.float32).astype(jnp.bfloat16)
    rolled = jnp.roll(own_rows, -level_half, axis=0)
    incoming = from_behind(rolled[:, :, :lon_half], "lon", -1)
    rolled = jnp.concatenate([rolled[:, :, lon_half:], incoming], axis=2)
    incoming = from_behind(rolled[:, :lat_half], "lat", -1)
    projections = jnp.concatenate([rolled[:, lat_half:], incoming], axis=1)
    bias_full = earth_bias(bias_table, index_table)
    allowed = window_rules(levels, lat_start, lat_rows, lat_total, pad_mask)
    attended = from_windows(attend(to_windows(projections), bias_full, allowed))
    incoming = from_behind(attended[:, -lat_half:], "lat", 1)
    returned = jnp.concatenate([incoming, attended[:, :-lat_half]], axis=1)
    incoming = from_behind(returned[:, :, -lon_half:], "lon", 1)
    returned = jnp.concatenate([incoming, returned[:, :, :-lon_half]], axis=2)
    normed = finish(returned, w_proj, proj_bias, norm_gain, norm_shift)
    normed = jnp.roll(normed, level_half, axis=0)
    return (hidden.astype(jnp.float32) + normed).astype(jnp.bfloat16)


def solution(mesh):
    in_specs = (
        P("member", "lat", "lon", None),
        P("lat", "lon"),
        P(),
        P(),
        P(),
        P(),
        P(),
        P(),
        P(),
        P("lat", None, None, None),
        P(),
    )
    out_specs = P("member", "lat", "lon", None)
    return jax.shard_map(
        on_device, mesh=mesh, in_specs=in_specs, out_specs=out_specs, check_vma=False
    )
```

profile of v0, /device:TPU:33, one launch (start us, length us, event | category | flops | bytes accessed | tf_op | source)
XLA Modules:
  0.0 206.8 jit_solution(1751742921675209416)
XLA Ops:
  0.0 0.0 copy-start
  0.0 0.9 slice_reduce_fusion.1
  0.9 0.7 broadcast_compare_fusion
  1.6 0.1 broadcast_select_fusion.2
  1.7 0.0 copy-start.2
  1.7 0.8 copy-done.2
  2.5 2.9 %convolution_convert_fusion = bf16[4,12,12,1152]{3,2,1,0:T(8,128)(2,1)S(1)} fusion(bf16[768,1152]{1,0:T(8,128)(2,1)S(1)} %copy-done, bf16[4,12,12,768]{3,0,2,1:T(4,128)(2,1)} %param.11, f32[12,12,768]{2,1,0:T(8,128)S(1)} %broadcast_select_fusion.2), kind=kOutput, calls=%fused_computation.12 | convolution fusion | flops 1021206528 | bytes 4423680 | tf_op jit(solution)/shard_map/dot_general | solution.py:135
  5.4 0.1 slice.74
  5.6 0.0 copy-start.10
  5.6 0.0 copy-start.5
  5.6 0.4 fusion.14
  6.0 0.3 copy.49
  6.3 48.5 %collective-permute-start = (bf16[4,12,6,1152]{3,0,2,1:T(4,128)(2,1)S(1)}, bf16[4,12,6,1152]{3,0,2,1:T(4,128)(2,1)S(1)}, u32[]{:S(2)}, u32[]{:S(2)}) collective-permute-start(bf16[4,12,6,1152]{3,0,2,1:T(4,128)(2,1)S(1)} %copy.49), channel_id=1, source_target_pairs={{0,254},{2,0},{4,2},{6,4},{8,6},{10,8},{12,10},{14,12},{16,14},{18... | collective-permute-start | bytes 1990664 | tf_op jit(solution)/shard_map/ppermute | solution.py:19
  54.9 0.1 and_select_fusion
  55.0 0.0 copy-done.10
  55.0 0.1 select_reduce_fusion
  55.1 0.2 reshape.255
  55.3 0.3 fusion.34
  55.6 12.8 %collective-permute-done = bf16[4,12,6,1152]{3,0,2,1:T(4,128)(2,1)S(1)} collective-permute-done((bf16[4,12,6,1152]{3,0,2,1:T(4,128)(2,1)S(1)}, bf16[4,12,6,1152]{3,0,2,1:T(4,128)(2,1)S(1)}, u32[]{:S(2)}, u32[]{:S(2)}) %collective-permute-start) | collective-permute-done | bytes 663584 | tf_op jit(solution)/shard_map/ppermute | solution.py:19
  68.5 0.1 copy.50
  68.6 0.9 pad_maximum_fusion.3
  69.5 3.6 %collective-permute-start.1 = (bf16[4,3,12,1152]{3,2,1,0:T(8,128)(2,1)}, bf16[4,3,12,1152]{3,2,1,0:T(8,128)(2,1)S(1)}, u32[]{:S(2)}, u32[]{:S(2)}) collective-permute-start(bf16[4,3,12,1152]{3,2,1,0:T(8,128)(2,1)} %pad_maximum_fusion.3), channel_id=1, source_target_pairs={{0,1},{1,0},{2,3},{3,2},{4,5},{5,4},{6,7},{7,6},{8,9},{9,8},{10,11... | collective-permute-start | bytes 995336 | tf_op jit(solution)/shard_map/ppermute | solution.py:19
  73.1 0.9 compare_and_fusion
  73.9 1.0 copy.56
  74.9 0.1 reshape.254
  75.1 0.4 copy.57
  75.5 42.0 %gather_fusion = bf16[20736,48]{1,0:T(8,128)(2,1)} fusion(bf16[3312,48]{1,0:T(8,128)(2,1)S(1)} %bitcast.63, s32[21504]{0:T(1024)S(1)} %pad_clamp_fusion), kind=kCustom, calls=%fused_computation | custom fusion | bytes 4064256 | tf_op jit(solution)/shard_map/jit(_take)/gather | solution.py:56
  117.5 6.0 %copy.58 = bf16[20736,48]{0,1:T(8,128)(2,1)} copy(bf16[20736,48]{1,0:T(8,128)(2,1)} %gather_fusion) | data formatting | bytes 3981312 | tf_op jit(solution)/shard_map/jit(_take)/gather | solution.py:56
  123.5 8.2 %gather.7 = bf16[144,144,2,2,12]{1,0,4,3,2:T(8,128)(2,1)} reshape(bf16[20736,48]{0,1:T(8,128)(2,1)} %copy.58) | data formatting | bytes 3981312 | tf_op jit(solution)/shard_map/jit(_take)/gather | solution.py:56
  131.7 6.2 %copy.59 = bf16[144,144,2,2,12]{0,1,4,2,3:T(8,128)(2,1)} copy(bf16[144,144,2,2,12]{1,0,4,3,2:T(8,128)(2,1)} %gather.7) | data formatting | bytes 3981312 | tf_op jit(solution)/shard_map/jit(_take)/gather | solution.py:56
  137.9 0.1 copy.55
  138.1 0.4 fusion.12
  138.5 0.0 collective-permute-done.1
  138.5 0.3 pad_maximum_fusion
  138.8 1.0 copy.75
  139.9 6.7 %reshape_reshape.6 = bf16[2,2,1,144,3,12,32]{6,5,4,1,3,0,2:T(8,128)(2,1)} reshape(bf16[2,2,1,2,6,12,1152]{6,1,5,4,3,0,2:T(2,128)(2,1)S(1)} %bitcast.65) | data formatting | bytes 2654208 | tf_op jit(solution)/shard_map/reshape;reshape | solution.py:88
  146.6 6.7 %fusion.47 = (bf16[2,2,1,144,1,12,32]{6,5,4,1,3,0,2:T(8,128)(2,1)}, bf16[2,2,1,144,1,12,32]{6,5,4,1,3,0,2:T(8,128)(2,1)}, bf16[2,2,1,144,1,12,32]{6,5,4,1,3,0,2:T(8,128)(2,1)}) fusion(bf16[2,2,1,144,3,12,32]{6,5,4,1,3,0,2:T(8,128)(2,1)} %reshape_reshape.6), kind=kLoop, calls=%fused_computation.86 | loop fusion | bytes 2654208 | tf_op jit(solution)/shard_map/slice | solution.py:91
  153.2 3.3 %copy.68 = bf16[2,2,1,144,1,12,32]{3,6,5,1,0,4,2:T(8,128)(2,1)S(1)} copy(bf16[2,2,1,144,1,12,32]{6,5,4,1,3,0,2:T(8,128)(2,1)} %get-tuple-element.8) | data formatting | bytes 884736
  156.6 3.4 %copy.69 = bf16[2,2,1,144,1,12,32]{3,6,5,1,0,4,2:T(8,128)(2,1)S(1)} copy(bf16[2,2,1,144,1,12,32]{6,5,4,1,3,0,2:T(8,128)(2,1)} %get-tuple-element.9) | data formatting | bytes 884736
  160.0 0.0 copy-start.6
  160.0 3.6 %copy.67 = bf16[2,2,1,144,1,12,32]{3,6,5,1,0,4,2:T(8,128)(2,1)S(1)} copy(bf16[2,2,1,144,1,12,32]{6,5,4,1,3,0,2:T(8,128)(2,1)} %get-tuple-element.7) | data formatting | bytes 884736
  163.6 8.1 %fusion.48 = (f32[2,2,12,144]{3,2,1,0:T(8,128)S(1)}, f32[2,2,12,144,144]{3,4,2,1,0:T(8,128)}) fusion(pred[2,2,144,144]{2,3,1,0:T(8,128)(4,1)S(1)} %copy-done.6, bf16[144,144,2,2,12]{0,1,4,2,3:T(8,128)(2,1)} %copy.59, pred[144,144]{0,1:T(8,128)(4,1)S(1)} %copy.55, bf16[2,2,1,144,1,12,32]{3,6,5,1,0,4,2:T(8,128)(2,1)S(1)} %copy.69, ...), kind=kOutput, calls=%fused_computation.87 | convolution fusion | flops 70668432 | bytes 6988032 | tf_op jit(solution)/shard_map/sub | solution.py:98
  171.7 3.6 %fusion.13 = bf16[2,2,1,144,12,32]{3,5,4,1,0,2:T(8,128)(2,1)S(1)} fusion(f32[2,2,12,144,144]{3,4,2,1,0:T(8,128)} %get-tuple-element.15, f32[2,2,12,144]{3,2,1,0:T(8,128)S(1)} %get-tuple-element.14, bf16[2,2,1,144,1,12,32]{3,6,5,1,0,4,2:T(8,128)(2,1)S(1)} %copy.67), kind=kOutput, calls=%fused_computation.29 | convolution fusion | flops 65912832 | bytes 4893696 | tf_op jit(solution)/shard_map/abchtu,abcuhd->abcthd/dot_general | solution.py:100
  175.3 4.2 %copy.61 = bf16[2,2,1,144,12,32]{5,4,1,3,0,2:T(8,128)(2,1)} copy(bf16[2,2,1,144,12,32]{3,5,4,1,0,2:T(8,128)(2,1)S(1)} %fusion.13) | data formatting | bytes 884736 | tf_op jit(solution)/shard_map/convert_element_type | solution.py:102
  179.5 3.7 %reshape_reshape.7 = bf16[2,2,1,2,6,12,384]{6,1,5,4,3,0,2:T(2,128)(2,1)S(1)} reshape(bf16[2,2,1,144,12,32]{5,4,1,3,0,2:T(8,128)(2,1)} %copy.61) | data formatting | bytes 884736 | tf_op jit(solution)/shard_map/reshape;reshape | solution.py:80
  183.2 0.1 copy.62
  183.3 2.0 collective-permute-start.2
  185.3 1.3 collective-permute-done.2
  186.6 0.1 fusion.33
  186.7 0.0 copy-start.8
  186.8 0.0 copy-start.9
  186.8 2.0 collective-permute-start.3
  188.7 12.7 %collective-permute-done.3 = bf16[4,12,6,384]{3,2,1,0:T(8,128)(2,1)S(1)} collective-permute-done((bf16[4,12,6,384]{3,2,1,0:T(8,128)(2,1)S(1)}, bf16[4,12,6,384]{3,2,1,0:T(8,128)(2,1)S(1)}, u32[]{:S(2)}, u32[]{:S(2)}) %collective-permute-start.3) | collective-permute-done | bytes 221216 | tf_op jit(solution)/shard_map/ppermute | solution.py:19
  201.5 0.9 add_reduce_fusion
  202.4 0.5 multiply_reduce_fusion
  202.9 0.5 multiply_add_fusion
  203.4 0.0 copy-start.3
  203.4 0.0 copy-start.4
  203.4 0.1 slice.88
  203.5 0.0 copy-start.1
  203.6 0.9 copy-done.3
  204.5 0.3 copy-done.4
  204.7 0.4 fusion.8
  205.2 1.6 copy.63
  (24 shorter events, 0.3 us)
Async XLA Ops:
  0.0 2.5 %copy-start = (bf16[768,1152]{1,0:T(8,128)(2,1)S(1)}, bf16[768,1152]{1,0:T(8,128)(2,1)}, u32[]{:S(2)}) copy-start(bf16[768,1152]{1,0:T(8,128)(2,1)} %param.15) | copy-start | bytes 5308420
  1.7 0.8 copy-start.2
  5.6 49.4 %copy-start.10 = (s32[24]{0:T(128)S(1)}, s32[24]{0:T(128)}, u32[]{:S(2)}) copy-start(s32[24]{0:T(128)} %param.13) | copy-start | bytes 292
  5.6 49.5 %copy-start.5 = (s32[144,144]{1,0:T(8,128)S(1)}, s32[144,144]{1,0:T(8,128)}, u32[]{:S(2)}) copy-start(s32[144,144]{1,0:T(8,128)} %param.21) | copy-start | bytes 248836
  6.3 62.1 %collective-permute-start = (bf16[4,12,6,1152]{3,0,2,1:T(4,128)(2,1)S(1)}, bf16[4,12,6,1152]{3,0,2,1:T(4,128)(2,1)S(1)}, u32[]{:S(2)}, u32[]{:S(2)}) collective-permute-start(bf16[4,12,6,1152]{3,0,2,1:T(4,128)(2,1)S(1)} %copy.49), channel_id=1, source_target_pairs={{0,254},{2,0},{4,2},{6,4},{8,6},{10,8},{12,10},{14,12},{16,14},{18... | collective-permute-start | bytes 1990664 | tf_op jit(solution)/shard_map/ppermute | solution.py:19
  69.5 69.0 %collective-permute-start.1 = (bf16[4,3,12,1152]{3,2,1,0:T(8,128)(2,1)}, bf16[4,3,12,1152]{3,2,1,0:T(8,128)(2,1)S(1)}, u32[]{:S(2)}, u32[]{:S(2)}) collective-permute-start(bf16[4,3,12,1152]{3,2,1,0:T(8,128)(2,1)} %pad_maximum_fusion.3), channel_id=1, source_target_pairs={{0,1},{1,0},{2,3},{3,2},{4,5},{5,4},{6,7},{7,6},{8,9},{9,8},{10,11... | collective-permute-start | bytes 995336 | tf_op jit(solution)/shard_map/ppermute | solution.py:19
  160.0 3.6 %copy-start.6 = (pred[2,2,144,144]{2,3,1,0:T(8,128)(4,1)S(1)}, pred[2,2,144,144]{2,3,1,0:T(8,128)(4,1)}, u32[]{:S(2)}) copy-start(pred[2,2,144,144]{2,3,1,0:T(8,128)(4,1)} %compare_and_fusion) | copy-start | bytes 248836
  179.5 22.0 %copy-start.7 = (f32[768]{0:T(1024)S(1)}, f32[768]{0:T(1024)}, u32[]{:S(2)}) copy-start(f32[768]{0:T(1024)} %param.17) | copy-start | bytes 9220
  179.5 22.0 %copy-start.11 = (bf16[384,768]{1,0:T(8,128)(2,1)S(1)}, bf16[384,768]{1,0:T(8,128)(2,1)}, u32[]{:S(2)}) copy-start(bf16[384,768]{1,0:T(8,128)(2,1)} %param.16) | copy-start | bytes 1769476
  183.3 3.3 %collective-permute-start.2 = (bf16[4,3,12,384]{3,2,1,0:T(8,128)(2,1)S(1)}, bf16[4,3,12,384]{3,2,1,0:T(8,128)(2,1)S(1)}, u32[]{:S(2)}, u32[]{:S(2)}) collective-permute-start(bf16[4,3,12,384]{3,2,1,0:T(8,128)(2,1)S(1)} %slice.83), channel_id=1, source_target_pairs={{0,1},{1,0},{2,3},{3,2},{4,5},{5,4},{6,7},{7,6},{8,9},{9,8},{10,11... | collective-permute-start | bytes 331784 | tf_op jit(solution)/shard_map/ppermute | solution.py:19
  186.7 16.1 %copy-start.8 = (f32[768]{0:T(1024)S(1)}, f32[768]{0:T(1024)}, u32[]{:S(2)}) copy-start(f32[768]{0:T(1024)} %param.19) | copy-start | bytes 9220
  186.8 16.1 %copy-start.9 = (f32[768]{0:T(1024)S(1)}, f32[768]{0:T(1024)}, u32[]{:S(2)}) copy-start(f32[768]{0:T(1024)} %param.18) | copy-start | bytes 9220
  186.8 14.7 %collective-permute-start.3 = (bf16[4,12,6,384]{3,2,1,0:T(8,128)(2,1)S(1)}, bf16[4,12,6,384]{3,2,1,0:T(8,128)(2,1)S(1)}, u32[]{:S(2)}, u32[]{:S(2)}) collective-permute-start(bf16[4,12,6,384]{3,2,1,0:T(8,128)(2,1)S(1)} %fusion.33), channel_id=1, source_target_pairs={{0,2},{2,4},{4,6},{6,8},{8,10},{10,12},{12,14},{14,16},{16,18},{18... | collective-permute-start | bytes 663560 | tf_op jit(solution)/shard_map/ppermute | solution.py:19
  203.4 1.1 copy-start.3
  203.4 1.3 copy-start.4
  203.5 3.3 %copy-start.1 = (bf16[768,1152]{1,0:T(8,128)(2,1)S(1)}, bf16[768,1152]{1,0:T(8,128)(2,1)}, u32[]{:S(2)}) copy-start(bf16[768,1152]{1,0:T(8,128)(2,1)} %param.15) | copy-start | bytes 5308420
where the time goes:
time: 208 us; the launch traced here: 207 us
  local copies, waits for them, and re-layouts  102 us (49%)
  starting transfers between devices  56 us (27%)
  waiting for transfers between devices  26.8 us (13%)
  matrix products  15.5 us (7%)
  other arithmetic  5.85 us (3%)
    gather x4, local copies, waits for them, and re-layouts, earth_bias(): picked = jnp.take(table_rows, index_table.reshape(-1), axis=0)  62.4 us
    ppermute x4, starting transfers between devices, from_behind(): lax.ppermute(shard, axis, [(i, (i + by) % size) for i in range(size)])  56 us
    ppermute x4, waiting for transfers between devices, from_behind(): lax.ppermute(shard, axis, [(i, (i + by) % size) for i in range(size)])  26.8 us
    unnamed x28, local copies, waits for them, and re-layouts  13.3 us
    sub x1, matrix products, attend(): powers = jnp.exp(scores - largest)  8.11 us
    another operation x1, local copies, waits for them, and re-layouts, attend(): pieces = windows.reshape(windows.shape[:-1] + (3, HEADS, HEAD_DIM))  6.7 us
    slice x1, local copies, waits for them, and re-layouts, attend(): value_rows = pieces[..., 2, :, :]  6.66 us
    convert_element_type x1, local copies, waits for them, and re-layouts, attend(): attended = jnp.einsum('abchtu,abcuhd->abcthd', weights, value_rows, prefe...  4.18 us
  transfers between devices with their start and end apart: 4, of which 3 were waited for; matrix products, arithmetic and copies ran while one was open for 32% of the time, Pallas kernels for 0%

commit v1 on v0

v1 whole, which is shorter than its diff:
```python
import functools

import jax
import jax.numpy as jnp
from jax import lax
from jax.experimental import pallas as pl
from jax.experimental.pallas import tpu as pltpu
from jax.sharding import PartitionSpec as P

HEADS = 12
HEAD_DIM = 32
WIDTH = HEADS * HEAD_DIM
WIN_Z = 2
WIN_LAT = 6
WIN_LON = 12
WIN_TOK = 144
HALF = 72
PIECE = 18
GROUP = 4
GROUPS = HEADS // GROUP
T_STEP = 16
SPAN = 256
NEG = -1e30

norm_epsilon = 1e-05

MESH = pl.DeviceIdType.MESH
F32 = jnp.float32
BF16 = jnp.bfloat16


def nt_dot(a, b):
    return lax.dot_general(a, b, (((1,), (1,)), ((), ())), preferred_element_type=F32)


def kernel(
    lat_total,
    blocks,
    state_ref,
    land_ref,
    embed_ref,
    index_ref,
    bias_table_ref,
    w_qkv_hbm,
    w_proj_hbm,
    proj_bias_ref,
    gain_ref,
    shift_ref,
    pad_ref,
    out_ref,
    tokens,
    m0_ref,
    m1_ref,
    ed_ref,
    table32,
    table_ref,
    ordered,
    idx_ref,
    w_qkv,
    w_proj,
    edge_in,
    halo0,
    halo1,
    haloe,
    q_buf,
    kv_buf,
    acc,
    bias,
    att0,
    att1,
    atte,
    atte_out,
    atte_in,
    w_sem,
    lat_send,
    lat_recv,
    lon_send,
    lon_recv,
):
    member = lax.axis_index("member")
    lon = lax.axis_index("lon")
    lat = lax.axis_index("lat")
    lon_size = lax.axis_size("lon")
    left = (member, lax.rem(lon + lon_size - 1, lon_size), lat)
    right = (member, lax.rem(lon + 1, lon_size), lat)
    partner = (member, lon, 1 - lat)

    wq_copy = pltpu.make_async_copy(w_qkv_hbm, w_qkv, w_sem.at[0])
    wq_copy.start()
    wp_copy = pltpu.make_async_copy(w_proj_hbm, w_proj, w_sem.at[1])
    wp_copy.start()

    barrier = pltpu.get_barrier_semaphore()
    for other in (left, right, partner):
        pl.semaphore_signal(barrier, inc=1, device_id=other, device_id_type=MESH)

    levels = state_ref.shape[0]
    eye = (
        lax.broadcasted_iota(jnp.int32, (WIN_LON, WIN_LON), 0)
        == lax.broadcasted_iota(jnp.int32, (WIN_LON, WIN_LON), 1)
    )
    land = nt_dot(jnp.where(eye, 1.0, 0.0).astype(BF16), land_ref[...].astype(F32).astype(BF16))

    def place_of(level, r):
        rolled = (level + levels - 1) % levels
        if r < 3:
            return 12 * PIECE + rolled * PIECE + r * 6
        if r < 9:
            return rolled * 2 * PIECE + (r - 3) * 6
        return 8 * PIECE + rolled * PIECE + (r - 9) * 6

    def prepare(row_range):
        for r in row_range:
            embedded = jnp.where(land[:, r : r + 1] == 1.0, embed_ref[1:2, :], embed_ref[0:1, :])
            for level in range(levels):
                full = state_ref[level, r].astype(F32) + embedded
                place = place_of(level, r)
                for half in range(2):
                    tokens[half, place : place + 6, :] = full[half * 6 : half * 6 + 6]

    prepare(range(3))
    ed_ref[...] = tokens[:, 12 * PIECE :, :].astype(BF16)
    prepare(range(9, 12))
    m1_ref[...] = tokens[:, 8 * PIECE : 12 * PIECE, :].astype(BF16)
    pl.semaphore_wait(barrier, 3)

    def remote(src, dst, send, recv, to):
        return pltpu.make_async_remote_copy(
            src_ref=src, dst_ref=dst, send_sem=send, recv_sem=recv, device_id=to, device_id_type=MESH
        )

    edge_copy = remote(ed_ref, edge_in, lat_send.at[0], lat_recv.at[0], partner)
    edge_copy.start()

    def lon_copies(own, halo, k):
        return [
            remote(own.at[0], halo.at[1], lon_send.at[2 * k], lon_recv.at[2 * k], left),
            remote(own.at[1], halo.at[0], lon_send.at[2 * k + 1], lon_recv.at[2 * k + 1], right),
        ]

    copies1 = lon_copies(m1_ref, halo1, 0)
    copiese = lon_copies(edge_in, haloe, 1)
    copies0 = lon_copies(m0_ref, halo0, 2)
    for c in copies1:
        c.start()

    prepare(range(3, 9))
    m0_ref[...] = tokens[:, : 8 * PIECE, :].astype(BF16)

    rows = 2 * 2 * HEADS
    positions = bias_table_ref.shape[3]
    for z in range(2):
        for b in range(2):
            for k in range(blocks):
                place = k * rows + (z * 2 + b) * HEADS
                stop = min(positions, (k + 1) * SPAN)
                part = bias_table_ref[b, z, :, k * SPAN : stop].astype(F32)
                if stop < (k + 1) * SPAN:
                    part = jnp.concatenate([part, jnp.zeros((HEADS, (k + 1) * SPAN - stop), F32)], axis=1)
                table32[place : place + HEADS, :] = part
    table_ref[...] = table32[...].astype(BF16)

    new = lax.broadcasted_iota(jnp.int32, (WIN_TOK, WIN_TOK), 0)
    old = lax.broadcasted_iota(jnp.int32, (WIN_TOK, WIN_TOK), 1)
    inside = new % HALF
    order = jnp.where(old == inside // 6 * WIN_LON + new // HALF * 6 + inside % 6, 1.0, 0.0).astype(BF16)

    def reorder(x):
        x = jnp.dot(order, x.astype(F32).astype(BF16), preferred_element_type=F32)
        return nt_dot(x.astype(BF16), order)

    index = index_ref[...]
    ordered[...] = (reorder(index >> 8) * SPAN + reorder(index & (SPAN - 1))).astype(jnp.int32)
    steps = WIN_TOK // T_STEP
    for i in range(T_STEP):
        idx_ref[:, i * WIN_TOK : (i + 1) * WIN_TOK] = ordered[i * steps : (i + 1) * steps, :]

    def bias_step(step, carry):
        for j in range(T_STEP * WIN_TOK // 256):
            lanes = slice(j * 256, (j + 1) * 256)
            picked = idx_ref[pl.ds(step, 1), lanes]
            low = jnp.broadcast_to(picked & (SPAN - 1), (SPAN, 256))
            hot = jnp.where(lax.broadcasted_iota(jnp.int32, (SPAN, 256), 0) == low, 1.0, 0.0).astype(BF16)
            high = jnp.broadcast_to(picked >> 8, (rows, 256))
            found = jnp.dot(table_ref[...], hot, preferred_element_type=F32)
            total = found[:rows]
            for k in range(1, blocks):
                total = jnp.where(high == k, found[k * rows : (k + 1) * rows], total)
            acc[:, lanes] = total
        for i in range(T_STEP):
            for c in range(2):
                offset = i * WIN_TOK + c * HALF
                base = offset // 128 * 128
                shift = offset - base
                if shift + HALF <= 128:
                    piece = acc[:, base : base + 128]
                    if shift:
                        piece = pltpu.roll(piece, 128 - shift, 1)
                else:
                    piece = pltpu.roll(acc[:, base : base + 256], 256 - shift, 1)[:, :128]
                bias[c, pl.ds(i * steps + step, rows, stride=WIN_TOK), :] = piece
        return carry

    edge_copy.wait_recv()
    for c in copiese:
        c.start()
    for c in copies0:
        c.start()

    lax.fori_loop(0, steps, bias_step, 0)

    wq_copy.wait()

    def rounded(x):
        return x.astype(BF16).astype(F32)

    def put_main(slot, both):
        for a in range(2):
            kv_buf[slot, a, 0] = both[a * HALF : (a + 1) * HALF]

    def put_piece(slot, both, rh):
        for level in range(4):
            start = (level % 2) * 2 * PIECE + rh * PIECE
            kv_buf[slot, level // 2, 1, start : start + PIECE, :] = both[level * PIECE : (level + 1) * PIECE]

    def put_query(half, both, rh):
        for level in range(4):
            start = (level % 2) * 2 * PIECE + rh * PIECE
            q_buf[half, level // 2, 1, start : start + PIECE, :] = both[level * PIECE : (level + 1) * PIECE]

    features = w_qkv.shape[0]
    own = jnp.concatenate(
        [ref[...].reshape(-1, features) for ref in (m0_ref, m1_ref, edge_in)], axis=0
    )
    full = rounded(jnp.dot(own, w_qkv[...], preferred_element_type=F32))
    for half in range(2):
        main = full[half * 2 * HALF : (half + 1) * 2 * HALF]
        for a in range(2):
            q_buf[half, a, 0] = main[a * HALF : (a + 1) * HALF, :WIDTH]
        put_main(half + 1, main[:, WIDTH:])
        for rh in range(2):
            part = full[(4 + 2 * rh + half) * HALF : (5 + 2 * rh + half) * HALF]
            put_query(half, part[:, :WIDTH], rh)
            put_piece(half + 1, part[:, WIDTH:], rh)

    lane = lax.broadcasted_iota(jnp.int32, (HALF, 128), 1)
    row = lax.broadcasted_iota(jnp.int32, (HALF, 128), 0)
    lane_head = lane // HEAD_DIM
    lat_start = lat * 2 * WIN_LAT

    def attend(a, b, half):
        valid = lane < HALF
        same_z = jnp.logical_or(a == 0, (lane // 36) == (row // 36))
        wraps = lat_start + b * WIN_LAT >= lat_total - WIN_LAT
        same_r = jnp.logical_or(jnp.logical_not(wraps), (lane // PIECE) % 2 == (row // PIECE) % 2)
        lane_row = lane % 36 // WIN_LAT
        usable = jnp.zeros((HALF, 128), jnp.int32)
        for r in range(WIN_LAT):
            value = pad_ref[lax.rem(lat_start + b * WIN_LAT + r + WIN_LAT // 2, lat_total)]
            usable = jnp.where(lane_row == r, value, usable)
        allowed = valid & same_z & same_r & (usable == 1)
        slot0 = 2 * half
        out = []
        zeros = jnp.zeros((128 - HALF, 128), F32)
        ones = jnp.ones((256, 128), BF16)
        query_half = 1 - half
        for g in range(GROUPS):
            cols = slice(g * 128, (g + 1) * 128)
            vcols = slice(WIDTH + g * 128, WIDTH + (g + 1) * 128)
            q = q_buf[half, a, b, :, cols]
            stacked = jnp.concatenate([jnp.where(lane_head == h, q, 0.0) for h in range(GROUP)], axis=0).astype(BF16)
            keys = jnp.concatenate(
                [kv_buf[slot0, a, b, :, cols], zeros, kv_buf[slot0 + 1, a, b, :, cols], zeros], axis=0
            ).astype(BF16)
            values = jnp.concatenate(
                [kv_buf[slot0, a, b, :, vcols], zeros, kv_buf[slot0 + 1, a, b, :, vcols], zeros], axis=0
            ).astype(BF16)
            values = jnp.concatenate([values, ones], axis=1)
            scores = nt_dot(stacked, keys)
            powers = []
            for h in range(GROUP):
                first = ((a * 2 + b) * HEADS + g * GROUP + h) * WIN_TOK + query_half * HALF
                parts = []
                for c in range(2):
                    s = scores[h * HALF : (h + 1) * HALF, c * 128 : (c + 1) * 128] * (HEAD_DIM**-0.5)
                    s = s + bias[c, pl.ds(pl.multiple_of(first, 8), HALF), :]
                    parts.append(jnp.where(allowed, s, NEG))
                largest = jnp.max(jnp.maximum(parts[0], parts[1]), axis=1, keepdims=True)
                powers.append(jnp.concatenate([jnp.exp(p - largest) for p in parts], axis=1))
            weights = jnp.concatenate(powers, axis=0).astype(BF16)
            product = jnp.dot(weights, values, preferred_element_type=F32)
            top = jnp.zeros((HALF, 128), F32)
            bottom = jnp.zeros((HALF, 128), F32)
            for h in range(GROUP):
                part = product[h * HALF : (h + 1) * HALF]
                top = jnp.where(lane_head == h, part[:, :128], top)
                bottom = jnp.where(lane_head == h, part[:, 128:], bottom)
            out.append(top / bottom)
        return jnp.concatenate(out, axis=1)

    for c in copies1 + copiese:
        c.wait_recv()
    other = jnp.concatenate([ref[...].reshape(-1, features) for ref in (halo1, haloe)], axis=0)
    full = rounded(jnp.dot(other, w_qkv[:, WIDTH:], preferred_element_type=F32))
    for c in range(2):
        for rh in range(2):
            put_piece(3 * c, full[(2 * rh + c) * HALF : (2 * rh + c + 1) * HALF], rh)

    def edge_unit(half, carry):
        for a in range(2):
            result = attend(a, 1, half)
            for k in range(2):
                att1[half, (2 * a + k) * PIECE : (2 * a + k + 1) * PIECE, :] = result[2 * k * PIECE : (2 * k + 1) * PIECE]
                atte[half, (2 * a + k) * PIECE : (2 * a + k + 1) * PIECE, :] = result[
                    (2 * k + 1) * PIECE : (2 * k + 2) * PIECE
                ]
        return carry

    lax.fori_loop(0, 2, edge_unit, 0)
    atte_out[...] = atte[...].astype(BF16)
    return_copy = remote(atte_out, atte_in, lat_send.at[1], lat_recv.at[1], partner)
    return_copy.start()

    for c in copies0:
        c.wait_recv()
    full = rounded(jnp.dot(halo0[...].reshape(-1, features), w_qkv[:, WIDTH:], preferred_element_type=F32))
    for c in range(2):
        put_main(3 * c, full[c * 2 * HALF : (c + 1) * 2 * HALF])

    def main_unit(unit, carry):
        half = unit % 2
        a = unit // 2
        att0[half, pl.ds(pl.multiple_of(a * HALF, 8), HALF), :] = attend(a, 0, half)
        return carry

    lax.fori_loop(0, 4, main_unit, 0)
    wp_copy.wait()

    def finish(attended, hidden):
        projected = jnp.dot(attended.astype(BF16), w_proj[...], preferred_element_type=F32) + proj_bias_ref[...][None]
        average = jnp.mean(projected, axis=-1, keepdims=True)
        centered = projected - average
        spread = jnp.mean(centered * centered, axis=-1, keepdims=True)
        normed = centered * lax.rsqrt(spread + norm_epsilon) * gain_ref[...][None] + shift_ref[...][None]
        return hidden.astype(F32) + normed

    def emit(row_range):
        for level in range(levels):
            for r in row_range:
                place = place_of(level, r)
                pair = [tokens[half, place : place + 6, :] for half in range(2)]
                out_ref[level, r] = jnp.concatenate(pair, axis=0).astype(BF16)

    for half in range(2):
        tokens[half, : 8 * PIECE] = finish(att0[half], m0_ref[half])
        tokens[half, 8 * PIECE : 12 * PIECE] = finish(att1[half], m1_ref[half])
    emit(range(3, 12))
    return_copy.wait_recv()
    for half in range(2):
        tokens[half, 12 * PIECE :] = finish(atte_in[half], ed_ref[half])
    emit(range(3))
    edge_copy.wait_send()
    return_copy.wait_send()
    for c in copies1 + copiese + copies0:
        c.wait_send()


def on_device(
    state_tokens,
    land_mask,
    pad_mask,
    land_embed,
    w_qkv,
    w_proj,
    proj_bias,
    norm_gain,
    norm_shift,
    bias_table,
    index_table,
):
    levels, lat_rows, lon_columns, features = state_tokens.shape
    lat_windows, z_windows, heads, positions = bias_table.shape
    lat_total = lat_rows * lax.axis_size("lat")
    half_columns = WIN_LON // 2
    blocks = -(-positions // SPAN)

    side = (2, levels * PIECE, features)
    main = (2, levels * 2 * PIECE, features)
    rows = z_windows * lat_windows * heads

    vmem = pl.BlockSpec(memory_space=pltpu.VMEM)
    anywhere = pl.BlockSpec(memory_space=pl.ANY)
    return pl.pallas_call(
        functools.partial(kernel, lat_total, blocks),
        out_shape=jax.ShapeDtypeStruct(state_tokens.shape, BF16),
        in_specs=[vmem] * 5 + [anywhere] * 2 + [vmem] * 3 + [pl.BlockSpec(memory_space=pltpu.SMEM)],
        out_specs=vmem,
        scratch_shapes=[
            pltpu.VMEM((2, 16 * PIECE, features), F32),
            pltpu.VMEM(main, BF16),
            pltpu.VMEM(side, BF16),
            pltpu.VMEM(side, BF16),
            pltpu.VMEM((blocks * rows, SPAN), F32),
            pltpu.VMEM((blocks * rows, SPAN), BF16),
            pltpu.VMEM((WIN_TOK, WIN_TOK), jnp.int32),
            pltpu.VMEM((WIN_TOK // T_STEP, T_STEP * WIN_TOK), jnp.int32),
            pltpu.VMEM(w_qkv.shape, BF16),
            pltpu.VMEM(w_proj.shape, BF16),
            pltpu.VMEM(side, BF16),
            pltpu.VMEM(main, BF16),
            pltpu.VMEM(side, BF16),
            pltpu.VMEM(side, BF16),
            pltpu.VMEM((2, 2, 2, HALF, WIDTH), F32),
            pltpu.VMEM((4, 2, 2, HALF, 2 * WIDTH), F32),
            pltpu.VMEM((rows, T_STEP * WIN_TOK + 128), F32),
            pltpu.VMEM((2, rows * WIN_TOK, 128), F32),
            pltpu.VMEM((2, 2 * HALF, WIDTH), F32),
            pltpu.VMEM((2, HALF, WIDTH), F32),
            pltpu.VMEM((2, HALF, WIDTH), F32),
            pltpu.VMEM((2, HALF, WIDTH), BF16),
            pltpu.VMEM((2, HALF, WIDTH), BF16),
            pltpu.SemaphoreType.DMA((2,)),
            pltpu.SemaphoreType.DMA((2,)),
            pltpu.SemaphoreType.DMA((2,)),
            pltpu.SemaphoreType.DMA((6,)),
            pltpu.SemaphoreType.DMA((6,)),
        ],
        compiler_params=pltpu.CompilerParams(
            collective_id=0, has_side_effects=True, vmem_limit_bytes=56 * 1024 * 1024
        ),
        name="window_layer",
    )(
        state_tokens,
        land_mask,
        land_embed,
        index_table,
        bias_table,
        w_qkv,
        w_proj,
        proj_bias,
        norm_gain,
        norm_shift,
        pad_mask,
    )


def solution(mesh):
    in_specs = (
        P("member", "lat", "lon", None),
        P("lat", "lon"),
        P(),
        P(),
        P(),
        P(),
        P(),
        P(),
        P(),
        P("lat", None, None, None),
        P(),
    )
    out_specs = P("member", "lat", "lon", None)
    return jax.shard_map(
        on_device, mesh=mesh, in_specs=in_specs, out_specs=out_specs, check_vma=False
    )
```

time: 208 us -> 79.1 us (0.38)
  local copies, waits for them, and re-layouts: 102 us -> 6.94 us
  Pallas kernels: 0 us -> 71.9 us
  starting transfers between devices: 56 us -> 0 us
  waiting for transfers between devices: 26.8 us -> 0 us
  matrix products: 15.5 us -> 0 us
  other arithmetic: 5.85 us -> 0 us
    pallas_call x0 -> x1, Pallas kernels: none -> 71.9 us  [on_device(): pl.pallas_call(functools.partial(kernel, lat_total, blocks), out_shape=ja...]
    gather x4 -> x0, local copies, waits for them, and re-layouts: 62.4 us -> none  [earth_bias(): picked = jnp.take(table_rows, index_table.reshape(-1), axis=0)]
    ppermute x4 -> x0, starting transfers between devices: 56 us -> none  [from_behind(): lax.ppermute(shard, axis, [(i, (i + by) % size) for i in range(size)])]
    ppermute x4 -> x0, waiting for transfers between devices: 26.8 us -> none  [from_behind(): lax.ppermute(shard, axis, [(i, (i + by) % size) for i in range(size)])]
    another operation x2 -> x0, local copies, waits for them, and re-layouts: 10.4 us -> none  [the longest x1 6.7 us: attend(): pieces = windows.reshape(windows.shape[:-1] + (3, HEADS, HEAD_DIM))]
    unnamed x28 -> x2, local copies, waits for them, and re-layouts: 13.3 us -> 4.08 us
    slice x9 -> x0, local copies, waits for them, and re-layouts: 8.22 us -> none  [the longest x1 6.66 us: attend(): value_rows = pieces[..., 2, :, :]]
    sub x1 -> x0, matrix products: 8.11 us -> none  [attend(): powers = jnp.exp(scores - largest)]
  transfers between devices with their start and end apart: 4 -> 0, of which waited for: 3 -> 0; matrix products, arithmetic and copies ran while one was open for 32% -> 0% of each run, Pallas kernels for 0% -> 0%
where the time goes in v1:
time: 79.1 us; the launch traced here: 78.9 us
  Pallas kernels  71.9 us (91%)
  local copies, waits for them, and re-layouts  6.94 us (9%)
    pallas_call x1, Pallas kernels, on_device(): pl.pallas_call(functools.partial(kernel, lat_total, blocks), out_shape=ja...  71.9 us
    unnamed x2, local copies, waits for them, and re-layouts  4.08 us
    pallas_call x1, local copies, waits for them, and re-layouts, on_device(): pl.pallas_call(functools.partial(kernel, lat_total, blocks), out_shape=ja...  2.87 us

profile of v1, /device:TPU:33, one launch (start us, length us, event | category | flops | bytes accessed | tf_op | source)
XLA Modules:
  0.0 78.9 jit_solution(3388286368673984195)
XLA Ops:
  0.0 1.8 %copy.13.bias_table_ref = bf16[2,2,12,3312]{3,2,1,0:T(8,128)(2,1)} copy(bf16[2,2,12,3312]{3,1,2,0:T(2,128)(2,1)} %param.20) | data formatting | bytes 635904 | tf_op args[9]
  1.8 2.3 %copy.12.state_ref = bf16[4,12,12,768]{3,2,1,0:T(8,128)(2,1)} copy(bf16[4,12,12,768]{3,0,2,1:T(4,128)(2,1)} %param.11) | data formatting | bytes 1769472 | tf_op args[0]
  4.1 71.9 %window_layer.1 = bf16[4,12,12,768]{3,2,1,0:T(8,128)(2,1)} custom-call(bf16[4,12,12,768]{3,2,1,0:T(8,128)(2,1)} %copy.12.state_ref, s32[12,12]{1,0:T(8,128)} %land_ref.1, f32[2,768]{1,0:T(2,128)} %embed_ref.1, s32[144,144]{1,0:T(8,128)} %index_ref.1, bf16[2,2,12,3312]{3,2,1,0:T(8,128)(2,1)} %copy.13.bias_table_ref, bf16[768,1152]{1,0:T(8,128)(2,1)} %w_qkv_hbm.1, ...), custom_call_target="tpu_custom_call" | custom-call | tf_op jit(solution)/shard_map/window_layer/pallas_call | solution.py:393
  76.0 2.9 %copy.14 = bf16[4,12,12,768]{3,0,2,1:T(4,128)(2,1)} copy(bf16[4,12,12,768]{3,2,1,0:T(8,128)(2,1)} %window_layer.1) | data formatting | bytes 1769472 | tf_op jit(solution)/shard_map/window_layer/pallas_call | solution.py:393

commit v2 on v1

--- a/solution.py
+++ b/solution.py
@@ -36,17 +36,25 @@
 def kernel(
     lat_total,
     blocks,
+    state_hbm,
+    embed_hbm,
+    index_hbm,
+    bias_table_hbm,
+    w_qkv_hbm,
+    w_proj_hbm,
+    proj_bias_hbm,
+    gain_hbm,
+    shift_hbm,
+    land_ref,
+    pad_ref,
+    out_hbm,
     state_ref,
-    land_ref,
     embed_ref,
     index_ref,
     bias_table_ref,
-    w_qkv_hbm,
-    w_proj_hbm,
     proj_bias_ref,
     gain_ref,
     shift_ref,
-    pad_ref,
     out_ref,
     tokens,
     m0_ref,
@@ -72,6 +80,7 @@
     atte_out,
     atte_in,
     w_sem,
+    out_sem,
     lat_send,
     lat_recv,
     lon_send,
@@ -85,43 +94,65 @@
     right = (member, lax.rem(lon + 1, lon_size), lat)
     partner = (member, lon, 1 - lat)
 
-    wq_copy = pltpu.make_async_copy(w_qkv_hbm, w_qkv, w_sem.at[0])
-    wq_copy.start()
-    wp_copy = pltpu.make_async_copy(w_proj_hbm, w_proj, w_sem.at[1])
-    wp_copy.start()
-
     barrier = pltpu.get_barrier_semaphore()
     for other in (left, right, partner):
         pl.semaphore_signal(barrier, inc=1, device_id=other, device_id_type=MESH)
 
-    levels = state_ref.shape[0]
-    eye = (
-        lax.broadcasted_iota(jnp.int32, (WIN_LON, WIN_LON), 0)
-        == lax.broadcasted_iota(jnp.int32, (WIN_LON, WIN_LON), 1)
-    )
-    land = nt_dot(jnp.where(eye, 1.0, 0.0).astype(BF16), land_ref[...].astype(F32).astype(BF16))
-
-    def place_of(level, r):
-        rolled = (level + levels - 1) % levels
+    loads = [
+        pltpu.make_async_copy(src, dst, w_sem.at[k])
+        for k, (src, dst) in enumerate(
+            [
+                (embed_hbm, embed_ref),
+                (state_hbm, state_ref),
+                (index_hbm, index_ref),
+                (bias_table_hbm, bias_table_ref),
+                (w_qkv_hbm, w_qkv),
+                (w_proj_hbm, w_proj),
+                (proj_bias_hbm, proj_bias_ref),
+                (gain_hbm, gain_ref),
+                (shift_hbm, shift_ref),
+            ]
+        )
+    ]
+    for load in loads:
+        load.start()
+
+    levels = state_ref.shape[2]
+
+    def place_of(r, half, c):
         if r < 3:
-            return 12 * PIECE + rolled * PIECE + r * 6
+            return 12 * PIECE + r * 6 + c, PIECE
         if r < 9:
-            return rolled * 2 * PIECE + (r - 3) * 6
-        return 8 * PIECE + rolled * PIECE + (r - 9) * 6
+            return (r - 3) * 6 + c, 2 * PIECE
+        return 8 * PIECE + (r - 9) * 6 + c, PIECE
+
+    loads[0].wait()
+    loads[1].wait()
+    sea = jnp.broadcast_to(embed_ref[0:1, :], (levels, embed_ref.shape[1]))
+    ground = jnp.broadcast_to(embed_ref[1:2, :], (levels, embed_ref.shape[1]))
 
     def prepare(row_range):
         for r in row_range:
-            embedded = jnp.where(land[:, r : r + 1] == 1.0, embed_ref[1:2, :], embed_ref[0:1, :])
-            for level in range(levels):
-                full = state_ref[level, r].astype(F32) + embedded
-                place = place_of(level, r)
-                for half in range(2):
-                    tokens[half, place : place + 6, :] = full[half * 6 : half * 6 + 6]
+            for half in range(2):
+                for c in range(6):
+                    column = half * 6 + c
+                    embedded = jnp.where(land_ref[r, column] == 1, ground, sea)
+                    full = state_ref[r, column].astype(F32) + embedded
+                    place, step = place_of(r, half, c)
+                    for k in range(0, full.shape[1], 128):
+                        tokens[half, k // 128, pl.ds(place, levels, stride=step), :] = full[:, k : k + 128]
+
+    def joined(half, start, stop):
+        return jnp.concatenate([tokens[half, k, start:stop, :] for k in range(tokens.shape[1])], axis=1)
+
+    def gathered(ref, start, stop):
+        for half in range(2):
+            ref[half] = joined(half, start, stop).astype(BF16)
 
     prepare(range(3))
-    ed_ref[...] = tokens[:, 12 * PIECE :, :].astype(BF16)
+    gathered(ed_ref, 12 * PIECE, 16 * PIECE)
     prepare(range(9, 12))
-    m1_ref[...] = tokens[:, 8 * PIECE : 12 * PIECE, :].astype(BF16)
+    gathered(m1_ref, 8 * PIECE, 12 * PIECE)
     pl.semaphore_wait(barrier, 3)
 
     def remote(src, dst, send, recv, to):
@@ -145,20 +176,22 @@
         c.start()
 
     prepare(range(3, 9))
-    m0_ref[...] = tokens[:, : 8 * PIECE, :].astype(BF16)
+    gathered(m0_ref, 0, 8 * PIECE)
 
     rows = 2 * 2 * HEADS
     positions = bias_table_ref.shape[3]
-    for z in range(2):
-        for b in range(2):
-            for k in range(blocks):
-                place = k * rows + (z * 2 + b) * HEADS
-                stop = min(positions, (k + 1) * SPAN)
-                part = bias_table_ref[b, z, :, k * SPAN : stop].astype(F32)
-                if stop < (k + 1) * SPAN:
-                    part = jnp.concatenate([part, jnp.zeros((HEADS, (k + 1) * SPAN - stop), F32)], axis=1)
-                table32[place : place + HEADS, :] = part
-    table_ref[...] = table32[...].astype(BF16)
+    loads[3].wait()
+    for b in range(2):
+        for h in range(HEADS):
+            both = bias_table_ref[b, h].astype(F32)
+            for k in range(blocks * SPAN // 128):
+                place = k // 2 * rows + b * HEADS + h
+                stop = min(positions, (k + 1) * 128)
+                part = both[:, k * 128 : stop]
+                if stop < (k + 1) * 128:
+                    part = jnp.concatenate([part, jnp.zeros((2, (k + 1) * 128 - stop), F32)], axis=1)
+                table32[k % 2, pl.ds(place, 2, stride=2 * HEADS), :] = part
+    table_ref[...] = jnp.concatenate([table32[0], table32[1]], axis=1).astype(BF16)
 
     new = lax.broadcasted_iota(jnp.int32, (WIN_TOK, WIN_TOK), 0)
     old = lax.broadcasted_iota(jnp.int32, (WIN_TOK, WIN_TOK), 1)
@@ -169,6 +202,7 @@
         x = jnp.dot(order, x.astype(F32).astype(BF16), preferred_element_type=F32)
         return nt_dot(x.astype(BF16), order)
 
+    loads[2].wait()
     index = index_ref[...]
     ordered[...] = (reorder(index >> 8) * SPAN + reorder(index & (SPAN - 1))).astype(jnp.int32)
     steps = WIN_TOK // T_STEP
@@ -209,24 +243,38 @@
 
     lax.fori_loop(0, steps, bias_step, 0)
 
-    wq_copy.wait()
+    loads[4].wait()
 
     def rounded(x):
         return x.astype(BF16).astype(F32)
 
     def put_main(slot, both):
-        for a in range(2):
-            kv_buf[slot, a, 0] = both[a * HALF : (a + 1) * HALF]
+        for level in range(4):
+            rolled = (level + 3) % 4
+            start = (rolled % 2) * 2 * PIECE
+            kv_buf[slot, rolled // 2, 0, start : start + 2 * PIECE, :] = both[
+                level * 2 * PIECE : (level + 1) * 2 * PIECE
+            ]
 
     def put_piece(slot, both, rh):
         for level in range(4):
-            start = (level % 2) * 2 * PIECE + rh * PIECE
-            kv_buf[slot, level // 2, 1, start : start + PIECE, :] = both[level * PIECE : (level + 1) * PIECE]
+            rolled = (level + 3) % 4
+            start = (rolled % 2) * 2 * PIECE + rh * PIECE
+            kv_buf[slot, rolled // 2, 1, start : start + PIECE, :] = both[level * PIECE : (level + 1) * PIECE]
+
+    def put_query_main(half, both):
+        for level in range(4):
+            rolled = (level + 3) % 4
+            start = (rolled % 2) * 2 * PIECE
+            q_buf[half, rolled // 2, 0, start : start + 2 * PIECE, :] = both[
+                level * 2 * PIECE : (level + 1) * 2 * PIECE
+            ]
 
     def put_query(half, both, rh):
         for level in range(4):
-            start = (level % 2) * 2 * PIECE + rh * PIECE
-            q_buf[half, level // 2, 1, start : start + PIECE, :] = both[level * PIECE : (level + 1) * PIECE]
+            rolled = (level + 3) % 4
+            start = (rolled % 2) * 2 * PIECE + rh * PIECE
+            q_buf[half, rolled // 2, 1, start : start + PIECE, :] = both[level * PIECE : (level + 1) * PIECE]
 
     features = w_qkv.shape[0]
     own = jnp.concatenate(
@@ -235,8 +283,7 @@
     full = rounded(jnp.dot(own, w_qkv[...], preferred_element_type=F32))
     for half in range(2):
         main = full[half * 2 * HALF : (half + 1) * 2 * HALF]
-        for a in range(2):
-            q_buf[half, a, 0] = main[a * HALF : (a + 1) * HALF, :WIDTH]
+        put_query_main(half, main[:, :WIDTH])
         put_main(half + 1, main[:, WIDTH:])
         for rh in range(2):
             part = full[(4 + 2 * rh + half) * HALF : (5 + 2 * rh + half) * HALF]
@@ -310,10 +357,9 @@
         for a in range(2):
             result = attend(a, 1, half)
             for k in range(2):
-                att1[half, (2 * a + k) * PIECE : (2 * a + k + 1) * PIECE, :] = result[2 * k * PIECE : (2 * k + 1) * PIECE]
-                atte[half, (2 * a + k) * PIECE : (2 * a + k + 1) * PIECE, :] = result[
-                    (2 * k + 1) * PIECE : (2 * k + 2) * PIECE
-                ]
+                place = (2 * a + k + 1) % 4 * PIECE
+                att1[half, place : place + PIECE, :] = result[2 * k * PIECE : (2 * k + 1) * PIECE]
+                atte[half, place : place + PIECE, :] = result[(2 * k + 1) * PIECE : (2 * k + 2) * PIECE]
         return carry
 
     lax.fori_loop(0, 2, edge_unit, 0)
@@ -327,14 +373,17 @@
     for c in range(2):
         put_main(3 * c, full[c * 2 * HALF : (c + 1) * 2 * HALF])
 
-    def main_unit(unit, carry):
-        half = unit % 2
-        a = unit // 2
-        att0[half, pl.ds(pl.multiple_of(a * HALF, 8), HALF), :] = attend(a, 0, half)
+    def main_unit(half, carry):
+        for a in range(2):
+            result = attend(a, 0, half)
+            for k in range(2):
+                place = (2 * a + k + 1) % 4 * 2 * PIECE
+                att0[half, place : place + 2 * PIECE, :] = result[k * 2 * PIECE : (k + 1) * 2 * PIECE]
         return carry
 
-    lax.fori_loop(0, 4, main_unit, 0)
-    wp_copy.wait()
+    lax.fori_loop(0, 2, main_unit, 0)
+    for load in loads[5:]:
+        load.wait()
 
     def finish(attended, hidden):
         projected = jnp.dot(attended.astype(BF16), w_proj[...], preferred_element_type=F32) + proj_bias_ref[...][None]
@@ -344,25 +393,38 @@
         normed = centered * lax.rsqrt(spread + norm_epsilon) * gain_ref[...][None] + shift_ref[...][None]
         return hidden.astype(F32) + normed
 
+    def keep(half, start, values):
+        for k in range(tokens.shape[1]):
+            tokens[half, k, start : start + values.shape[0], :] = values[:, k * 128 : (k + 1) * 128]
+
     def emit(row_range):
-        for level in range(levels):
-            for r in row_range:
-                place = place_of(level, r)
-                pair = [tokens[half, place : place + 6, :] for half in range(2)]
-                out_ref[level, r] = jnp.concatenate(pair, axis=0).astype(BF16)
+        for r in row_range:
+            for half in range(2):
+                for c in range(6):
+                    place, step = place_of(r, half, c)
+                    found = [tokens[half, k, pl.ds(place, levels, stride=step), :] for k in range(tokens.shape[1])]
+                    out_ref[r, half * 6 + c] = jnp.concatenate(found, axis=1).astype(BF16)
 
     for half in range(2):
-        tokens[half, : 8 * PIECE] = finish(att0[half], m0_ref[half])
-        tokens[half, 8 * PIECE : 12 * PIECE] = finish(att1[half], m1_ref[half])
+        keep(half, 0, finish(att0[half], m0_ref[half]))
+        keep(half, 8 * PIECE, finish(att1[half], m1_ref[half]))
     emit(range(3, 12))
+    stores = [
+        pltpu.make_async_copy(out_ref.at[pl.ds(first, size)], out_hbm.at[pl.ds(first, size)], out_sem.at[k])
+        for k, (first, size) in enumerate([(3, 9), (0, 3)])
+    ]
+    stores[0].start()
     return_copy.wait_recv()
     for half in range(2):
-        tokens[half, 12 * PIECE :] = finish(atte_in[half], ed_ref[half])
+        keep(half, 12 * PIECE, finish(atte_in[half], ed_ref[half]))
     emit(range(3))
+    stores[1].start()
     edge_copy.wait_send()
     return_copy.wait_send()
     for c in copies1 + copiese + copies0:
         c.wait_send()
+    for store in stores:
+        store.wait()
 
 
 def on_device(
@@ -388,19 +450,29 @@
     main = (2, levels * 2 * PIECE, features)
     rows = z_windows * lat_windows * heads
 
-    vmem = pl.BlockSpec(memory_space=pltpu.VMEM)
+    state = state_tokens.transpose(1, 2, 0, 3)
+    tables = bias_table.transpose(0, 2, 1, 3)
     anywhere = pl.BlockSpec(memory_space=pl.ANY)
-    return pl.pallas_call(
+    smem = pl.BlockSpec(memory_space=pltpu.SMEM)
+    result = pl.pallas_call(
         functools.partial(kernel, lat_total, blocks),
-        out_shape=jax.ShapeDtypeStruct(state_tokens.shape, BF16),
-        in_specs=[vmem] * 5 + [anywhere] * 2 + [vmem] * 3 + [pl.BlockSpec(memory_space=pltpu.SMEM)],
-        out_specs=vmem,
+        out_shape=jax.ShapeDtypeStruct(state.shape, BF16),
+        in_specs=[anywhere] * 9 + [smem] * 2,
+        out_specs=anywhere,
         scratch_shapes=[
-            pltpu.VMEM((2, 16 * PIECE, features), F32),
+            pltpu.VMEM(state.shape, BF16),
+            pltpu.VMEM(land_embed.shape, F32),
+            pltpu.VMEM(index_table.shape, jnp.int32),
+            pltpu.VMEM(tables.shape, BF16),
+            pltpu.VMEM(proj_bias.shape, F32),
+            pltpu.VMEM(norm_gain.shape, F32),
+            pltpu.VMEM(norm_shift.shape, F32),
+            pltpu.VMEM(state.shape, BF16),
+            pltpu.VMEM((2, features // 128, 16 * PIECE, 128), F32),
             pltpu.VMEM(main, BF16),
             pltpu.VMEM(side, BF16),
             pltpu.VMEM(side, BF16),
-            pltpu.VMEM((blocks * rows, SPAN), F32),
+            pltpu.VMEM((2, blocks * rows, 128), F32),
             pltpu.VMEM((blocks * rows, SPAN), BF16),
             pltpu.VMEM((WIN_TOK, WIN_TOK), jnp.int32),
             pltpu.VMEM((WIN_TOK // T_STEP, T_STEP * WIN_TOK), jnp.int32),
@@ -419,6 +491,7 @@
             pltpu.VMEM((2, HALF, WIDTH), F32),
             pltpu.VMEM((2, HALF, WIDTH), BF16),
             pltpu.VMEM((2, HALF, WIDTH), BF16),
+            pltpu.SemaphoreType.DMA((9,)),
             pltpu.SemaphoreType.DMA((2,)),
             pltpu.SemaphoreType.DMA((2,)),
             pltpu.SemaphoreType.DMA((2,)),
@@ -430,18 +503,19 @@
         ),
         name="window_layer",
     )(
-        state_tokens,
-        land_mask,
+        state,
         land_embed,
         index_table,
-        bias_table,
+        tables,
         w_qkv,
         w_proj,
         proj_bias,
         norm_gain,
         norm_shift,
+        land_mask,
         pad_mask,
     )
+    return result.transpose(2, 0, 1, 3)
 
 
 def solution(mesh):

time: 79.1 us -> 72.5 us (0.917)
  local copies, waits for them, and re-layouts: 6.94 us -> 2.38 us
  Pallas kernels: 71.9 us -> 69.9 us
    pallas_call x1 -> x0, local copies, waits for them, and re-layouts: 2.87 us -> none  [on_device(): pl.pallas_call(functools.partial(kernel, lat_total, blocks), out_shape=ja...]
    pallas_call x1, Pallas kernels: 71.9 us -> 69.9 us  [on_device(): pl.pallas_call(functools.partial(kernel, lat_total, blocks), out_shape=ja...]
    unnamed x2 -> x1, local copies, waits for them, and re-layouts: 4.08 us -> 2.38 us
where the time goes in v2:
time: 72.5 us; the launch traced here: 72.3 us
  Pallas kernels  69.9 us (96%)
  local copies, waits for them, and re-layouts  2.38 us (3%)
    pallas_call x1, Pallas kernels, on_device(): pl.pallas_call(functools.partial(kernel, lat_total, blocks), out_shape=ja...  69.9 us
    unnamed x1, local copies, waits for them, and re-layouts  2.38 us

profile of v2, /device:TPU:33, one launch (start us, length us, event | category | flops | bytes accessed | tf_op | source)
XLA Modules:
  0.0 72.3 jit_solution(10198190876809441279)
XLA Ops:
  0.0 69.9 %window_layer.1 = bf16[12,12,4,768]{3,2,1,0:T(4,128)(2,1)} custom-call(bf16[12,12,4,768]{3,2,1,0:T(4,128)(2,1)} %bitcast.4, f32[2,768]{1,0:T(2,128)} %embed_hbm.1, s32[144,144]{1,0:T(8,128)} %index_hbm.1, bf16[2,12,2,3312]{3,2,1,0:T(2,128)(2,1)} %bitcast.5, bf16[768,1152]{1,0:T(8,128)(2,1)} %w_qkv_hbm.1, bf16[384,768]{1,0:T(8,128)(2,1)} %w_proj_hbm.1, ...), custom_call_target="tpu_custom_call" | custom-call | tf_op jit(solution)/shard_map/window_layer/pallas_call | solution.py:457
  69.9 2.4 %copy.13 = bf16[4,12,12,768]{3,0,2,1:T(4,128)(2,1)} copy(bf16[4,12,12,768]{3,0,2,1:T(4,128)(2,1)} %bitcast.3) | data formatting | bytes 1769472

commit v3 on v2

--- a/solution.py
+++ b/solution.py
@@ -18,6 +18,7 @@
 PIECE = 18
 GROUP = 4
 GROUPS = HEADS // GROUP
+UNROLL = 9
 T_STEP = 16
 SPAN = 256
 NEG = -1e30
@@ -63,6 +64,7 @@
     table32,
     table_ref,
     ordered,
+    masks,
     idx_ref,
     w_qkv,
     w_proj,
@@ -114,7 +116,7 @@
             ]
         )
     ]
-    for load in loads:
+    for load in loads[:2]:
         load.start()
 
     levels = state_ref.shape[2]
@@ -128,6 +130,8 @@
 
     loads[0].wait()
     loads[1].wait()
+    for load in loads[2:]:
+        load.start()
     sea = jnp.broadcast_to(embed_ref[0:1, :], (levels, embed_ref.shape[1]))
     ground = jnp.broadcast_to(embed_ref[1:2, :], (levels, embed_ref.shape[1]))
 
@@ -178,62 +182,127 @@
     prepare(range(3, 9))
     gathered(m0_ref, 0, 8 * PIECE)
 
-    rows = 2 * 2 * HEADS
+    part_rows = table_ref.shape[0] // 2
+    tables = 2 * HEADS
     positions = bias_table_ref.shape[3]
     loads[3].wait()
+    spare = jnp.zeros((part_rows - blocks * tables, 128), F32)
+    for k in range(2):
+        for z in range(2):
+            table32[k, z * part_rows + blocks * tables : (z + 1) * part_rows, :] = spare
     for b in range(2):
         for h in range(HEADS):
             both = bias_table_ref[b, h].astype(F32)
             for k in range(blocks * SPAN // 128):
-                place = k // 2 * rows + b * HEADS + h
+                place = k // 2 * tables + b * HEADS + h
                 stop = min(positions, (k + 1) * 128)
                 part = both[:, k * 128 : stop]
                 if stop < (k + 1) * 128:
                     part = jnp.concatenate([part, jnp.zeros((2, (k + 1) * 128 - stop), F32)], axis=1)
-                table32[k % 2, pl.ds(place, 2, stride=2 * HEADS), :] = part
+                table32[k % 2, pl.ds(place, 2, stride=part_rows), :] = part
     table_ref[...] = jnp.concatenate([table32[0], table32[1]], axis=1).astype(BF16)
 
     new = lax.broadcasted_iota(jnp.int32, (WIN_TOK, WIN_TOK), 0)
     old = lax.broadcasted_iota(jnp.int32, (WIN_TOK, WIN_TOK), 1)
     inside = new % HALF
-    order = jnp.where(old == inside // 6 * WIN_LON + new // HALF * 6 + inside % 6, 1.0, 0.0).astype(BF16)
+    quarter = HALF // 2
+
+    def chosen(place):
+        return jnp.where(old == place, 1.0, 0.0).astype(BF16)
+
+    query_order = chosen(inside // 6 * WIN_LON + new // HALF * 6 + inside % 6)
+    key_order = chosen(new // HALF * HALF + inside % quarter // 6 * WIN_LON + inside // quarter * 6 + inside % 6)
 
     def reorder(x):
-        x = jnp.dot(order, x.astype(F32).astype(BF16), preferred_element_type=F32)
-        return nt_dot(x.astype(BF16), order)
+        x = jnp.dot(query_order, x.astype(F32).astype(BF16), preferred_element_type=F32)
+        return nt_dot(x.astype(BF16), key_order)
 
     loads[2].wait()
     index = index_ref[...]
-    ordered[...] = (reorder(index >> 8) * SPAN + reorder(index & (SPAN - 1))).astype(jnp.int32)
+    index = (reorder(index >> 8) * SPAN + reorder(index & (SPAN - 1))).astype(jnp.int32)
+    lower = lax.broadcasted_iota(jnp.int32, (WIN_TOK, HALF), 0) % HALF < quarter
+    ordered[0] = jnp.where(lower, index[:, :HALF], index[:, HALF:])
+    ordered[1] = jnp.where(lower, index[:, HALF:], index[:, :HALF])
     steps = WIN_TOK // T_STEP
+    spread = T_STEP * HALF
     for i in range(T_STEP):
-        idx_ref[:, i * WIN_TOK : (i + 1) * WIN_TOK] = ordered[i * steps : (i + 1) * steps, :]
-
-    def bias_step(step, carry):
-        for j in range(T_STEP * WIN_TOK // 256):
+        for other in range(2):
+            start = other * spread + i * HALF
+            idx_ref[:, start : start + HALF] = ordered[other, i * steps : (i + 1) * steps, :]
+
+    lane = lax.broadcasted_iota(jnp.int32, (HALF, 128), 1)
+    row = lax.broadcasted_iota(jnp.int32, (HALF, 128), 0)
+    lane_head = lane // HEAD_DIM
+    lat_start = lat * 2 * WIN_LAT
+    same_level = (lane // quarter) == (row // quarter)
+    same_rows = (lane // PIECE) % 2 == (row // PIECE) % 2
+    lane_row = lane % quarter // WIN_LAT
+    for b in range(2):
+        wraps = lat_start + b * WIN_LAT >= lat_total - WIN_LAT
+        usable = jnp.zeros((HALF, 128), jnp.int32)
+        for r in range(WIN_LAT):
+            value = pad_ref[lax.rem(lat_start + b * WIN_LAT + r + WIN_LAT // 2, lat_total)]
+            usable = jnp.where(lane_row == r, value, usable)
+        allowed = (lane < HALF) & (usable == 1) & jnp.logical_or(jnp.logical_not(wraps), same_rows)
+        masks[0, b] = jnp.where(allowed, 1, 0)
+        masks[1, b] = jnp.where(allowed & same_level, 1, 0)
+
+    first_part = lax.broadcasted_iota(jnp.int32, (tables, 128), 1) < quarter
+    width = 2 * spread
+
+    def bias_step(outer, carry):
+        for inner in range(UNROLL):
+            bias_rows(outer * UNROLL + inner, acc.at[inner])
+        return carry
+
+    def bias_rows(step, acc):
+        def find(j):
             lanes = slice(j * 256, (j + 1) * 256)
+            both = j * 256 < spread
             picked = idx_ref[pl.ds(step, 1), lanes]
             low = jnp.broadcast_to(picked & (SPAN - 1), (SPAN, 256))
             hot = jnp.where(lax.broadcasted_iota(jnp.int32, (SPAN, 256), 0) == low, 1.0, 0.0).astype(BF16)
-            high = jnp.broadcast_to(picked >> 8, (rows, 256))
-            found = jnp.dot(table_ref[...], hot, preferred_element_type=F32)
-            total = found[:rows]
-            for k in range(1, blocks):
-                total = jnp.where(high == k, found[k * rows : (k + 1) * rows], total)
-            acc[:, lanes] = total
-        for i in range(T_STEP):
+            high = jnp.broadcast_to(picked >> 8, (tables, 256))
+            entries = table_ref[...] if both else table_ref[:part_rows]
+            found = jnp.dot(entries, hot, preferred_element_type=F32)
+            for z in range(2 if both else 1):
+                start = z * part_rows
+                total = found[start : start + tables]
+                for k in range(1, blocks):
+                    total = jnp.where(high == k, found[start + k * tables : start + (k + 1) * tables], total)
+                acc[z, :, lanes] = total
+
+        def moved(z, source, target):
+            base = source // 128 * 128
+            shift = target - (source - base)
+            if source - base + quarter <= 128:
+                piece = acc[z, :, base : base + 128]
+                return pltpu.roll(piece, shift % 128, 1) if shift % 128 else piece
+            return pltpu.roll(acc[z, :, base : base + 256], shift % 256, 1)[:, :128]
+
+        def keep_row(i):
+            level = i // (T_STEP // 4) % 2
             for c in range(2):
-                offset = i * WIN_TOK + c * HALF
-                base = offset // 128 * 128
-                shift = offset - base
-                if shift + HALF <= 128:
-                    piece = acc[:, base : base + 128]
-                    if shift:
-                        piece = pltpu.roll(piece, 128 - shift, 1)
-                else:
-                    piece = pltpu.roll(acc[:, base : base + 256], 256 - shift, 1)[:, :128]
-                bias[c, pl.ds(i * steps + step, rows, stride=WIN_TOK), :] = piece
-        return carry
+                near = i * HALF + c * quarter
+                same = moved(0, near, level * quarter)
+                cross = moved(0, spread + near, (1 - level) * quarter)
+                pair = (same, cross) if level == 0 else (cross, same)
+                place = i * steps + step
+                bias[c, pl.ds(place, tables, stride=WIN_TOK), :] = jnp.where(first_part, *pair)
+                bias[c, pl.ds(tables * WIN_TOK + place, tables, stride=WIN_TOK), :] = moved(1, near, level * quarter)
+
+        done = set()
+        kept = 0
+        for j in (0, 4, 5, 1, 6, 2, 7, 3, 8):
+            find(j)
+            done.add(j)
+            while kept < T_STEP and all(
+                p // 256 in done
+                for start in (kept * HALF, spread + kept * HALF)
+                for p in range(start, start + HALF)
+            ):
+                keep_row(kept)
+                kept += 1
 
     edge_copy.wait_recv()
     for c in copiese:
@@ -241,7 +310,7 @@
     for c in copies0:
         c.start()
 
-    lax.fori_loop(0, steps, bias_step, 0)
+    lax.fori_loop(0, steps // UNROLL, bias_step, 0)
 
     loads[4].wait()
 
@@ -290,22 +359,8 @@
             put_query(half, part[:, :WIDTH], rh)
             put_piece(half + 1, part[:, WIDTH:], rh)
 
-    lane = lax.broadcasted_iota(jnp.int32, (HALF, 128), 1)
-    row = lax.broadcasted_iota(jnp.int32, (HALF, 128), 0)
-    lane_head = lane // HEAD_DIM
-    lat_start = lat * 2 * WIN_LAT
-
     def attend(a, b, half):
-        valid = lane < HALF
-        same_z = jnp.logical_or(a == 0, (lane // 36) == (row // 36))
-        wraps = lat_start + b * WIN_LAT >= lat_total - WIN_LAT
-        same_r = jnp.logical_or(jnp.logical_not(wraps), (lane // PIECE) % 2 == (row // PIECE) % 2)
-        lane_row = lane % 36 // WIN_LAT
-        usable = jnp.zeros((HALF, 128), jnp.int32)
-        for r in range(WIN_LAT):
-            value = pad_ref[lax.rem(lat_start + b * WIN_LAT + r + WIN_LAT // 2, lat_total)]
-            usable = jnp.where(lane_row == r, value, usable)
-        allowed = valid & same_z & same_r & (usable == 1)
+        allowed = masks[a, b] == 1
         slot0 = 2 * half
         out = []
         zeros = jnp.zeros((128 - HALF, 128), F32)
@@ -449,6 +504,7 @@
     side = (2, levels * PIECE, features)
     main = (2, levels * 2 * PIECE, features)
     rows = z_windows * lat_windows * heads
+    table_rows = -(-blocks * lat_windows * heads // 16) * 16
 
     state = state_tokens.transpose(1, 2, 0, 3)
     tables = bias_table.transpose(0, 2, 1, 3)
@@ -472,9 +528,10 @@
             pltpu.VMEM(main, BF16),
             pltpu.VMEM(side, BF16),
             pltpu.VMEM(side, BF16),
-            pltpu.VMEM((2, blocks * rows, 128), F32),
-            pltpu.VMEM((blocks * rows, SPAN), BF16),
-            pltpu.VMEM((WIN_TOK, WIN_TOK), jnp.int32),
+            pltpu.VMEM((2, z_windows * table_rows, 128), F32),
+            pltpu.VMEM((z_windows * table_rows, SPAN), BF16),
+            pltpu.VMEM((2, WIN_TOK, HALF), jnp.int32),
+            pltpu.VMEM((2, 2, HALF, 128), jnp.int32),
             pltpu.VMEM((WIN_TOK // T_STEP, T_STEP * WIN_TOK), jnp.int32),
             pltpu.VMEM(w_qkv.shape, BF16),
             pltpu.VMEM(w_proj.shape, BF16),
@@ -484,7 +541,7 @@
             pltpu.VMEM(side, BF16),
             pltpu.VMEM((2, 2, 2, HALF, WIDTH), F32),
             pltpu.VMEM((4, 2, 2, HALF, 2 * WIDTH), F32),
-            pltpu.VMEM((rows, T_STEP * WIN_TOK + 128), F32),
+            pltpu.VMEM((UNROLL, 2, lat_windows * heads, T_STEP * WIN_TOK + 128), F32),
             pltpu.VMEM((2, rows * WIN_TOK, 128), F32),
             pltpu.VMEM((2, 2 * HALF, WIDTH), F32),
             pltpu.VMEM((2, HALF, WIDTH), F32),

time: 72.5 us -> 68.6 us (0.946)
  Pallas kernels: 69.9 us -> 66 us
    pallas_call x1, Pallas kernels: 69.9 us -> 66 us  [on_device(): pl.pallas_call(functools.partial(kernel, lat_total, blocks), out_shape=ja...]
where the time goes in v3:
time: 68.6 us; the launch traced here: 68.4 us
  Pallas kernels  66 us (96%)
  local copies, waits for them, and re-layouts  2.38 us (3%)
    pallas_call x1, Pallas kernels, on_device(): pl.pallas_call(functools.partial(kernel, lat_total, blocks), out_shape=ja...  66 us
    unnamed x1, local copies, waits for them, and re-layouts  2.38 us

profile of v3, /device:TPU:33, one launch (start us, length us, event | category | flops | bytes accessed | tf_op | source)
XLA Modules:
  0.0 68.4 jit_solution(14934104866190498917)
XLA Ops:
  0.0 66.0 %window_layer.1 = bf16[12,12,4,768]{3,2,1,0:T(4,128)(2,1)} custom-call(bf16[12,12,4,768]{3,2,1,0:T(4,128)(2,1)} %bitcast.4, f32[2,768]{1,0:T(2,128)} %embed_hbm.1, s32[144,144]{1,0:T(8,128)} %index_hbm.1, bf16[2,12,2,3312]{3,2,1,0:T(2,128)(2,1)} %bitcast.5, bf16[768,1152]{1,0:T(8,128)(2,1)} %w_qkv_hbm.1, bf16[384,768]{1,0:T(8,128)(2,1)} %w_proj_hbm.1, ...), custom_call_target="tpu_custom_call" | custom-call | tf_op jit(solution)/shard_map/window_layer/pallas_call | solution.py:513
  66.0 2.4 %copy.13 = bf16[4,12,12,768]{3,0,2,1:T(4,128)(2,1)} copy(bf16[4,12,12,768]{3,0,2,1:T(4,128)(2,1)} %bitcast.3) | data formatting | bytes 1769472

commit v4 on v3

--- a/solution.py
+++ b/solution.py
@@ -18,7 +18,7 @@
 PIECE = 18
 GROUP = 4
 GROUPS = HEADS // GROUP
-UNROLL = 9
+NORM_ROWS = 48
 T_STEP = 16
 SPAN = 256
 NEG = -1e30
@@ -250,16 +250,11 @@
     first_part = lax.broadcasted_iota(jnp.int32, (tables, 128), 1) < quarter
     width = 2 * spread
 
-    def bias_step(outer, carry):
-        for inner in range(UNROLL):
-            bias_rows(outer * UNROLL + inner, acc.at[inner])
-        return carry
-
     def bias_rows(step, acc):
         def find(j):
             lanes = slice(j * 256, (j + 1) * 256)
             both = j * 256 < spread
-            picked = idx_ref[pl.ds(step, 1), lanes]
+            picked = idx_ref[step : step + 1, lanes]
             low = jnp.broadcast_to(picked & (SPAN - 1), (SPAN, 256))
             hot = jnp.where(lax.broadcasted_iota(jnp.int32, (SPAN, 256), 0) == low, 1.0, 0.0).astype(BF16)
             high = jnp.broadcast_to(picked >> 8, (tables, 256))
@@ -310,7 +305,8 @@
     for c in copies0:
         c.start()
 
-    lax.fori_loop(0, steps // UNROLL, bias_step, 0)
+    for step in range(steps):
+        bias_rows(step, acc.at[step])
 
     loads[4].wait()
 
@@ -408,16 +404,16 @@
         for rh in range(2):
             put_piece(3 * c, full[(2 * rh + c) * HALF : (2 * rh + c + 1) * HALF], rh)
 
-    def edge_unit(half, carry):
+    def edge_unit(half):
         for a in range(2):
             result = attend(a, 1, half)
             for k in range(2):
                 place = (2 * a + k + 1) % 4 * PIECE
                 att1[half, place : place + PIECE, :] = result[2 * k * PIECE : (2 * k + 1) * PIECE]
                 atte[half, place : place + PIECE, :] = result[(2 * k + 1) * PIECE : (2 * k + 2) * PIECE]
-        return carry
-
-    lax.fori_loop(0, 2, edge_unit, 0)
+
+    for half in range(2):
+        edge_unit(half)
     atte_out[...] = atte[...].astype(BF16)
     return_copy = remote(atte_out, atte_in, lat_send.at[1], lat_recv.at[1], partner)
     return_copy.start()
@@ -428,29 +424,33 @@
     for c in range(2):
         put_main(3 * c, full[c * 2 * HALF : (c + 1) * 2 * HALF])
 
-    def main_unit(half, carry):
+    def main_unit(half):
         for a in range(2):
             result = attend(a, 0, half)
             for k in range(2):
                 place = (2 * a + k + 1) % 4 * 2 * PIECE
                 att0[half, place : place + 2 * PIECE, :] = result[k * 2 * PIECE : (k + 1) * 2 * PIECE]
-        return carry
-
-    lax.fori_loop(0, 2, main_unit, 0)
+
+    for half in range(2):
+        main_unit(half)
     for load in loads[5:]:
         load.wait()
 
-    def finish(attended, hidden):
-        projected = jnp.dot(attended.astype(BF16), w_proj[...], preferred_element_type=F32) + proj_bias_ref[...][None]
-        average = jnp.mean(projected, axis=-1, keepdims=True)
-        centered = projected - average
-        spread = jnp.mean(centered * centered, axis=-1, keepdims=True)
-        normed = centered * lax.rsqrt(spread + norm_epsilon) * gain_ref[...][None] + shift_ref[...][None]
-        return hidden.astype(F32) + normed
-
-    def keep(half, start, values):
-        for k in range(tokens.shape[1]):
-            tokens[half, k, start : start + values.shape[0], :] = values[:, k * 128 : (k + 1) * 128]
+    proj_bias, gain, shift = (ref[...][None] for ref in (proj_bias_ref, gain_ref, shift_ref))
+
+    def finish(half, start, attended, hidden_ref):
+        projected = jnp.dot(attended.astype(BF16), w_proj[...], preferred_element_type=F32)
+        count = projected.shape[0]
+        for first in range(0, count, NORM_ROWS):
+            last = min(first + NORM_ROWS, count)
+            part = projected[first:last] + proj_bias
+            average = jnp.mean(part, axis=-1, keepdims=True)
+            centered = part - average
+            spread = jnp.mean(centered * centered, axis=-1, keepdims=True)
+            normed = centered * lax.rsqrt(spread + norm_epsilon) * gain + shift
+            total = hidden_ref[half, first:last].astype(F32) + normed
+            for k in range(tokens.shape[1]):
+                tokens[half, k, start + first : start + last, :] = total[:, k * 128 : (k + 1) * 128]
 
     def emit(row_range):
         for r in row_range:
@@ -461,8 +461,8 @@
                     out_ref[r, half * 6 + c] = jnp.concatenate(found, axis=1).astype(BF16)
 
     for half in range(2):
-        keep(half, 0, finish(att0[half], m0_ref[half]))
-        keep(half, 8 * PIECE, finish(att1[half], m1_ref[half]))
+        finish(half, 0, att0[half], m0_ref)
+        finish(half, 8 * PIECE, att1[half], m1_ref)
     emit(range(3, 12))
     stores = [
         pltpu.make_async_copy(out_ref.at[pl.ds(first, size)], out_hbm.at[pl.ds(first, size)], out_sem.at[k])
@@ -471,7 +471,7 @@
     stores[0].start()
     return_copy.wait_recv()
     for half in range(2):
-        keep(half, 12 * PIECE, finish(atte_in[half], ed_ref[half]))
+        finish(half, 12 * PIECE, atte_in[half], ed_ref)
     emit(range(3))
     stores[1].start()
     edge_copy.wait_send()
@@ -541,7 +541,7 @@
             pltpu.VMEM(side, BF16),
             pltpu.VMEM((2, 2, 2, HALF, WIDTH), F32),
             pltpu.VMEM((4, 2, 2, HALF, 2 * WIDTH), F32),
-            pltpu.VMEM((UNROLL, 2, lat_windows * heads, T_STEP * WIN_TOK + 128), F32),
+            pltpu.VMEM((WIN_TOK // T_STEP, 2, lat_windows * heads, T_STEP * WIN_TOK + 128), F32),
             pltpu.VMEM((2, rows * WIN_TOK, 128), F32),
             pltpu.VMEM((2, 2 * HALF, WIDTH), F32),
             pltpu.VMEM((2, HALF, WIDTH), F32),

time: 68.6 us -> 67.7 us (0.987)
  Pallas kernels: 66 us -> 65 us
    pallas_call x1, Pallas kernels: 66 us -> 65 us  [on_device(): pl.pallas_call(functools.partial(kernel, lat_total, blocks), out_shape=ja...]
where the time goes in v4:
time: 67.7 us; the launch traced here: 67.4 us
  Pallas kernels  65 us (96%)
  local copies, waits for them, and re-layouts  2.38 us (4%)
    pallas_call x1, Pallas kernels, on_device(): pl.pallas_call(functools.partial(kernel, lat_total, blocks), out_shape=ja...  65 us
    unnamed x1, local copies, waits for them, and re-layouts  2.38 us

profile of v4, /device:TPU:33, one launch (start us, length us, event | category | flops | bytes accessed | tf_op | source)
XLA Modules:
  0.0 67.4 jit_solution(4471034646642109540)
XLA Ops:
  0.0 65.0 %window_layer.1 = bf16[12,12,4,768]{3,2,1,0:T(4,128)(2,1)} custom-call(bf16[12,12,4,768]{3,2,1,0:T(4,128)(2,1)} %bitcast.4, f32[2,768]{1,0:T(2,128)} %embed_hbm.1, s32[144,144]{1,0:T(8,128)} %index_hbm.1, bf16[2,12,2,3312]{3,2,1,0:T(2,128)(2,1)} %bitcast.5, bf16[768,1152]{1,0:T(8,128)(2,1)} %w_qkv_hbm.1, bf16[384,768]{1,0:T(8,128)(2,1)} %w_proj_hbm.1, ...), custom_call_target="tpu_custom_call" | custom-call | tf_op jit(solution)/shard_map/window_layer/pallas_call | solution.py:513
  65.0 2.4 %copy.13 = bf16[4,12,12,768]{3,0,2,1:T(4,128)(2,1)} copy(bf16[4,12,12,768]{3,0,2,1:T(4,128)(2,1)} %bitcast.3) | data formatting | bytes 1769472
